TPU v7x, 512 devices: a whole 4x4x16 slice. The times are simulated.
512 devices in a mesh: row: 64 (over z, x), col: 8 (over y, core).
Axes of the slice: x: 4, y: 4, z: 16, core: 2. Of those that a mesh axis runs over, the one named last changes fastest.
Arguments:
- gate_up: bfloat16 [4, 2, 14336, 4096], P(None, None, 'row', 'col'), may hold values from -0.09375 to 0.09375
- down_weight: bfloat16 [4, 4096, 14336], P(None, 'row', 'col'), may hold values from -0.046875 to 0.046875
- query_output: bfloat16 [4, 2, 4096, 4096], P(None, None, 'row', 'col'), may hold values from -0.09375 to 0.09375
- probe_gate: bfloat16 [4, 2, 16, 4096], P(None, None, None, 'col'), may hold values from -6 to 6
- probe_down: bfloat16 [4, 16, 14336], P(None, None, 'col'), may hold values from -6 to 6
- probe_query: bfloat16 [4, 2, 16, 4096], P(None, None, None, 'col'), may hold values from -6 to 6
Outputs:
- vector_gate: float32 [4, 2, 16, 4096], P(None, None, None, 'col')
- vector_down: float32 [4, 16, 14336], P(None, None, 'col')
- vector_query: float32 [4, 2, 16, 4096], P(None, None, None, 'col')
- sigma_gate: float32 [4, 2, 16], replicated
- sigma_down: float32 [4, 16], replicated
- sigma_query: float32 [4, 2, 16], replicated
All inputs are finite; a program needn't handle non-finite values.
Results may differ from a plain program's by a relative error of at most 0.0033.
Values may be sent and summed in bfloat16 or wider, within the bound.
No kernel may reach another device: no remote copies, remote signals or barrier semaphores. Data moves between devices by JAX's collectives and lax.ppermute only.
A program may use at most 64 MiB of HBM per device.

v0:
```python
import jax
import jax.numpy as jnp
from jax import lax
from jax.sharding import Mesh
from jax.sharding import PartitionSpec as P

ITERS = 2
ROW = ("row_0", "row_1")
epsilon = 1e-06


def copy_for_each(shard, axis):
    length = lax.axis_size(axis)
    return lax.all_to_all(
        jnp.broadcast_to(shard[None], (length, *shard.shape)), axis, 0, 0, tiled=True
    )


def of_everyone(shard, axis):
    everything = copy_for_each(shard, axis)
    return jnp.sum(everything, axis=0)


def over_axes(shard, axes):
    for axis in axes:
        shard = lax.psum(shard, axis)
    return shard


def body(gate_up, down_weight, query_output, probe_gate, probe_down, probe_query):
    row_count = lax.axis_size(ROW)
    col_count = lax.axis_size("col")
    weights = (gate_up, down_weight[:, None], query_output)
    vectors = (probe_gate, probe_down[:, None], probe_query)
    scaled_right = vectors
    spectral = None

    def left_factor(total, weight):
        return lax.rsqrt(total[..., None] / (weight.shape[2] * row_count) + epsilon)

    for turn in range(ITERS):
        partial_value = tuple(
            (
                jnp.einsum("lmoi,lmki->lmko", weight, vector, preferred_element_type=jnp.float32)
                for weight, vector in zip(weights, vectors)
            )
        )
        summed = jax.tree.map(lambda part: of_everyone(part, "col"), partial_value)
        squares = tuple((jnp.sum(piece * piece, axis=3) for piece in summed))
        totals = jax.tree.map(lambda part: over_axes(part, ROW), squares)
        left_vecs = tuple((piece.astype(jnp.bfloat16) for piece in summed))
        right_partial = tuple(
            (
                jnp.einsum("lmoi,lmko->lmki", weight, left, preferred_element_type=jnp.float32)
                for weight, left in zip(weights, left_vecs)
            )
        )
        raw_sums = lax.psum(right_partial, ROW)
        right_sums = tuple(
            (
                raw * left_factor(total, weight)
                for raw, total, weight in zip(raw_sums, totals, weights)
            )
        )
        right_squares = tuple((jnp.sum(piece * piece, axis=3) for piece in right_sums))
        right_totals = jax.tree.map(lambda part: of_everyone(part, "col"), right_squares)
        scaled_right = tuple(
            (
                piece * lax.rsqrt(total[..., None] / (piece.shape[3] * col_count) + epsilon)
                for piece, total in zip(right_sums, right_totals)
            )
        )
        spectral = tuple(
            (
                jnp.sqrt(total / (weight.shape[2] * row_count))
                for weight, total in zip(weights, right_totals)
            )
        )
        vectors = tuple((piece.astype(jnp.bfloat16) for piece in scaled_right))
    return (
        scaled_right[0],
        scaled_right[1][:, 0],
        scaled_right[2],
        spectral[0],
        spectral[1][:, 0],
        spectral[2],
    )


def solution(mesh):
    finer = Mesh(mesh.devices.reshape(16, 4, mesh.shape["col"]), ("row_0", "row_1", "col"))
    in_specs = (
        P(None, None, ROW, "col"),
        P(None, ROW, "col"),
        P(None, None, ROW, "col"),
        P(None, None, None, "col"),
        P(None, None, "col"),
        P(None, None, None, "col"),
    )
    out_specs = (
        P(None, None, None, "col"),
        P(None, None, "col"),
        P(None, None, None, "col"),
        P(),
        P(),
        P(),
    )
    return jax.shard_map(body, mesh=finer, in_specs=in_specs, out_specs=out_specs, check_vma=False)
```

profile of v0, /device:TPU:1, one launch (start us, length us, event | category | flops | bytes accessed | tf_op | source)
XLA Modules:
  0.0 717.1 jit_solution(13803138326627123436)
XLA Ops:
  9.9 10.1 %all-to-all-start.4 = ((f32[8,1,4096]{2,1,0:T(1,128)}), f32[8,1,4096]{2,1,0:T(1,128)S(1)}, u32[]{:S(2)}, u32[]{:S(2)}) async-start(f32[8,1,4096]{2,1,0:T(1,128)} %reshape.197), calls=%async_computation.4 | async-start | bytes 262144 | tf_op jit(solution)/shard_map/all_to_all | solution.py:14
  21.3 3.9 all-to-all-done.4
  25.2 4.2 all-to-all-start.8
  30.7 5.2 all-to-all-done.8
  38.1 5.1 all-to-all-start
  61.1 45.7 %all-reduce.3 = (f32[4,2,16]{2,1,0:T(2,128)S(1)}, f32[4,1,16]{2,0,1:T(4,128)S(1)}, f32[4,2,16]{2,1,0:T(2,128)S(1)}) all-reduce(f32[4,2,16]{2,1,0:T(2,128)S(1)} %multiply_reduce_fusion.7, f32[4,1,16]{2,0,1:T(4,128)S(1)} %bitcast.30, f32[4,2,16]{2,1,0:T(2,128)S(1)} %multiply_reduce_fusion.9), channel_id=1, replica_groups=mesh['row_0'=16,'row_1'=4,'col'=8] {'row_0'}, use_global_device_ids=true, to_apply=%region_3.0 | all-reduce | flops 320 | bytes 2560 | tf_op jit(solution)/shard_map/psum | solution.py:26
  106.7 13.6 %all-reduce.5 = (f32[4,2,16]{2,1,0:T(2,128)S(1)}, f32[4,1,16]{2,0,1:T(4,128)S(1)}, f32[4,2,16]{2,1,0:T(2,128)S(1)}) all-reduce(f32[4,2,16]{2,1,0:T(2,128)S(1)} %get-tuple-element.15, f32[4,1,16]{2,0,1:T(4,128)S(1)} %get-tuple-element.16, f32[4,2,16]{2,1,0:T(2,128)S(1)} %get-tuple-element.17), channel_id=1, replica_groups=mesh['row_0'=16,'row_1'=4,'col'=8] {'row_1'}, use_global_device_ids=true, to_apply=%region_4.0 | all-reduce | flops 320 | bytes 2560 | tf_op jit(solution)/shard_map/psum | solution.py:26
  120.3 203.2 %all-reduce.11.cloned.1.call-done = (f32[4,2,16,512]{3,2,1,0:T(8,128)}, f32[4,1,16,1792]{3,2,0,1:T(8,128)}, f32[4,2,16,512]{3,2,1,0:T(8,128)}) async-done(((f32[4,2,16,512]{3,2,1,0:T(8,128)}, f32[4,1,16,1792]{3,2,0,1:T(8,128)}, f32[4,2,16,512]{3,2,1,0:T(8,128)}), (f32[4,2,16,512]{3,2,1,0:T(8,128)}, f32[4,1,16,1792]{3,2,0,1:T(8,128)}, f32[4,2,16,512]{3,2,1,0:T(8,128)})) %all-reduce.11.cloned.1.call-update) | async-done | bytes 983056 | tf_op jit(solution)/shard_map/psum | solution.py:58
  325.4 15.1 %all-to-all-start.5 = ((f32[8,4,1,16]{3,2,1,0:T(1,128)}), f32[8,4,1,16]{3,2,1,0:T(1,128)S(1)}, u32[]{:S(2)}, u32[]{:S(2)}) async-start(f32[8,4,1,16]{3,2,1,0:T(1,128)} %broadcast_in_dim.29), calls=%async_computation.5 | async-start | bytes 32768 | tf_op jit(solution)/shard_map/all_to_all | solution.py:14
  345.1 3.9 all-to-all-start.9
  354.2 4.3 all-to-all-start.1
  365.5 4.8 all-to-all-start.6
  372.4 3.3 all-to-all-done.6
  375.6 4.8 all-to-all-start.10
  381.7 5.3 all-to-all-done.10
  389.1 5.1 all-to-all-start.2
  394.2 2.4 reduce.13
  403.4 6.0 all-to-all-done.2
  412.1 41.4 %all-reduce.2 = (f32[4,2,16]{2,1,0:T(2,128)S(1)}, f32[4,1,16]{2,0,1:T(4,128)S(1)}, f32[4,2,16]{2,1,0:T(2,128)S(1)}) all-reduce(f32[4,2,16]{2,1,0:T(2,128)S(1)} %multiply_reduce_fusion.6, f32[4,1,16]{2,0,1:T(4,128)S(1)} %bitcast.31, f32[4,2,16]{2,1,0:T(2,128)S(1)} %multiply_reduce_fusion.8), channel_id=1, replica_groups=mesh['row_0'=16,'row_1'=4,'col'=8] {'row_0'}, use_global_device_ids=true, to_apply=%region_10.0 | all-reduce | flops 320 | bytes 2560 | tf_op jit(solution)/shard_map/psum | solution.py:26
  453.4 13.0 %all-reduce.4 = (f32[4,2,16]{2,1,0:T(2,128)S(1)}, f32[4,1,16]{2,0,1:T(4,128)S(1)}, f32[4,2,16]{2,1,0:T(2,128)S(1)}) all-reduce(f32[4,2,16]{2,1,0:T(2,128)S(1)} %get-tuple-element.12, f32[4,1,16]{2,0,1:T(4,128)S(1)} %get-tuple-element.13, f32[4,2,16]{2,1,0:T(2,128)S(1)} %get-tuple-element.14), channel_id=1, replica_groups=mesh['row_0'=16,'row_1'=4,'col'=8] {'row_1'}, use_global_device_ids=true, to_apply=%region_11.0 | all-reduce | flops 320 | bytes 2560 | tf_op jit(solution)/shard_map/psum | solution.py:26
  466.4 203.1 %all-reduce.9.cloned.1.call-done = (f32[4,2,16,512]{3,2,1,0:T(8,128)}, f32[4,1,16,1792]{3,2,0,1:T(8,128)}, f32[4,2,16,512]{3,2,1,0:T(8,128)}) async-done(((f32[4,2,16,512]{3,2,1,0:T(8,128)}, f32[4,1,16,1792]{3,2,0,1:T(8,128)}, f32[4,2,16,512]{3,2,1,0:T(8,128)}), (f32[4,2,16,512]{3,2,1,0:T(8,128)}, f32[4,1,16,1792]{3,2,0,1:T(8,128)}, f32[4,2,16,512]{3,2,1,0:T(8,128)})) %all-reduce.9.cloned.1.call-update) | async-done | bytes 983056 | tf_op jit(solution)/shard_map/psum | solution.py:58
  671.5 15.1 %all-to-all-start.7 = ((f32[8,4,1,16]{3,2,1,0:T(1,128)}), f32[8,4,1,16]{3,2,1,0:T(1,128)S(1)}, u32[]{:S(2)}, u32[]{:S(2)}) async-start(f32[8,4,1,16]{3,2,1,0:T(1,128)} %broadcast_in_dim.31), calls=%async_computation.7 | async-start | bytes 32768 | tf_op jit(solution)/shard_map/all_to_all | solution.py:14
  691.2 3.9 all-to-all-start.11
  699.7 3.9 all-to-all-start.3
  (123 shorter events, 76.3 us)
Async XLA Ops:
  7.2 22.3 %copy-start = (bf16[4,2,224,512]{3,2,1,0:T(8,128)(2,1)S(1)}, bf16[4,2,224,512]{3,2,1,0:T(8,128)(2,1)}, u32[]{:S(2)}) copy-start(bf16[4,2,224,512]{3,2,1,0:T(8,128)(2,1)} %param.6) | copy-start | bytes 5505028
  7.2 12.8 %copy-start.11 = (bf16[4,2,16,512]{3,2,1,0:T(8,128)(2,1)S(1)}, bf16[4,2,16,512]{3,2,1,0:T(8,128)(2,1)}, u32[]{:S(2)}) copy-start(bf16[4,2,16,512]{3,2,1,0:T(8,128)(2,1)} %param.11) | copy-start | bytes 393220
  7.2 12.8 %copy-start.2 = (bf16[4,2,64,512]{3,2,1,0:T(8,128)(2,1)S(1)}, bf16[4,2,64,512]{3,2,1,0:T(8,128)(2,1)}, u32[]{:S(2)}) copy-start(bf16[4,2,64,512]{3,2,1,0:T(8,128)(2,1)} %param.8) | copy-start | bytes 1572868
  9.0 20.4 %copy-start.10 = (bf16[4,2,16,512]{3,2,1,0:T(8,128)(2,1)S(1)}, bf16[4,2,16,512]{3,2,1,0:T(8,128)(2,1)}, u32[]{:S(2)}) copy-start(bf16[4,2,16,512]{3,2,1,0:T(8,128)(2,1)} %param.9) | copy-start | bytes 393220
  9.9 15.4 %all-to-all-start.4 = ((f32[8,1,4096]{2,1,0:T(1,128)}), f32[8,1,4096]{2,1,0:T(1,128)S(1)}, u32[]{:S(2)}, u32[]{:S(2)}) async-start(f32[8,1,4096]{2,1,0:T(1,128)} %reshape.197), calls=%async_computation.4 | async-start | bytes 262144 | tf_op jit(solution)/shard_map/all_to_all | solution.py:14
  25.2 4.2 copy-start.7
  25.2 10.7 %all-to-all-start.8 = ((f32[8,1,8192]{2,1,0:T(1,128)}), f32[8,1,8192]{2,1,0:T(1,128)S(1)}, u32[]{:S(2)}, u32[]{:S(2)}) async-start(f32[8,1,8192]{2,1,0:T(1,128)} %reshape.201), calls=%async_computation.8 | async-start | bytes 524288 | tf_op jit(solution)/shard_map/all_to_all | solution.py:14
  30.7 18.8 %copy-start.1 = (bf16[4,64,1792]{2,1,0:T(8,128)(2,1)S(1)}, bf16[4,64,1792]{2,1,0:T(8,128)(2,1)}, u32[]{:S(2)}) copy-start(bf16[4,64,1792]{2,1,0:T(8,128)(2,1)} %param.7) | copy-start | bytes 2752516
  35.9 12.0 %copy-start.4 = (f32[8,1,8192]{2,1,0:T(1,128)}, f32[8,1,8192]{2,1,0:T(1,128)S(1)}, u32[]{:S(2)}) copy-start(f32[8,1,8192]{2,1,0:T(1,128)S(1)} %all-to-all-done.8) | copy-start | bytes 786436
  38.1 20.2 %all-to-all-start = ((f32[8,4,2,16,224]{4,3,2,1,0:T(8,128)}), f32[8,4,2,16,224]{4,3,2,1,0:T(8,128)}, u32[]{:S(2)}, u32[]{:S(2)}) async-start(f32[8,4,2,16,224]{4,3,2,1,0:T(8,128)} %broadcast_in_dim.24), calls=%async_computation | async-start | bytes 2097152 | tf_op jit(solution)/shard_map/all_to_all | solution.py:14
  43.2 280.4 %all-reduce.11.cloned.1.call-start = ((), (), s32[]{:S(2)}) async-start(), calls=%async_computation.13 | async-start | bytes 1966080 | tf_op jit(solution)/shard_map/psum | solution.py:58
  325.4 19.7 %all-to-all-start.5 = ((f32[8,4,1,16]{3,2,1,0:T(1,128)}), f32[8,4,1,16]{3,2,1,0:T(1,128)S(1)}, u32[]{:S(2)}, u32[]{:S(2)}) async-start(f32[8,4,1,16]{3,2,1,0:T(1,128)} %broadcast_in_dim.29), calls=%async_computation.5 | async-start | bytes 32768 | tf_op jit(solution)/shard_map/all_to_all | solution.py:14
  345.1 8.5 %all-to-all-start.9 = ((f32[8,1,128]{2,1,0:T(1,128)}), f32[8,1,128]{2,1,0:T(1,128)S(1)}, u32[]{:S(2)}, u32[]{:S(2)}) async-start(f32[8,1,128]{2,1,0:T(1,128)} %reshape.203), calls=%async_computation.9 | async-start | bytes 8192 | tf_op jit(solution)/shard_map/all_to_all | solution.py:14
  351.3 29.1 %copy-start.3 = (f32[4,2,16,512]{3,2,1,0:T(8,128)S(1)}, f32[4,2,16,512]{3,2,1,0:T(8,128)}, u32[]{:S(2)}) copy-start(f32[4,2,16,512]{3,2,1,0:T(8,128)} %get-tuple-element.9) | copy-start | bytes 786436
  354.2 11.3 %all-to-all-start.1 = ((f32[8,1,128]{2,1,0:T(1,128)}), f32[8,1,128]{2,1,0:T(1,128)S(1)}, u32[]{:S(2)}, u32[]{:S(2)}) async-start(f32[8,1,128]{2,1,0:T(1,128)} %reshape.193), calls=%async_computation.1 | async-start | bytes 8192 | tf_op jit(solution)/shard_map/all_to_all | solution.py:14
  365.5 10.2 %all-to-all-start.6 = ((f32[8,1,4096]{2,1,0:T(1,128)}), f32[8,1,4096]{2,1,0:T(1,128)}, u32[]{:S(2)}, u32[]{:S(2)}) async-start(f32[8,1,4096]{2,1,0:T(1,128)} %reshape.199), calls=%async_computation.6 | async-start | bytes 262144 | tf_op jit(solution)/shard_map/all_to_all | solution.py:14
  375.6 11.4 %all-to-all-start.10 = ((f32[8,1,8192]{2,1,0:T(1,128)}), f32[8,1,8192]{2,1,0:T(1,128)}, u32[]{:S(2)}, u32[]{:S(2)}) async-start(f32[8,1,8192]{2,1,0:T(1,128)} %reshape.205), calls=%async_computation.10 | async-start | bytes 524288 | tf_op jit(solution)/shard_map/all_to_all | solution.py:14
  389.1 20.2 %all-to-all-start.2 = ((f32[8,4,2,16,224]{4,3,2,1,0:T(8,128)}), f32[8,4,2,16,224]{4,3,2,1,0:T(8,128)}, u32[]{:S(2)}, u32[]{:S(2)}) async-start(f32[8,4,2,16,224]{4,3,2,1,0:T(8,128)} %broadcast_in_dim.26), calls=%async_computation.2 | async-start | bytes 2097152 | tf_op jit(solution)/shard_map/all_to_all | solution.py:14
  394.2 275.3 %all-reduce.9.cloned.1.call-start = ((), (), s32[]{:S(2)}) async-start(), calls=%async_computation.12 | async-start | bytes 1966080 | tf_op jit(solution)/shard_map/psum | solution.py:58
  669.6 35.3 %copy-start.6 = (f32[4,2,16,512]{3,2,1,0:T(8,128)S(1)}, f32[4,2,16,512]{3,2,1,0:T(8,128)}, u32[]{:S(2)}) copy-start(f32[4,2,16,512]{3,2,1,0:T(8,128)} %get-tuple-element.8) | copy-start | bytes 786436
  669.6 39.9 %copy-start.5 = (f32[4,2,16,512]{3,2,1,0:T(8,128)S(1)}, f32[4,2,16,512]{3,2,1,0:T(8,128)}, u32[]{:S(2)}) copy-start(f32[4,2,16,512]{3,2,1,0:T(8,128)} %get-tuple-element.6) | copy-start | bytes 786436
  671.5 19.7 %all-to-all-start.7 = ((f32[8,4,1,16]{3,2,1,0:T(1,128)}), f32[8,4,1,16]{3,2,1,0:T(1,128)S(1)}, u32[]{:S(2)}, u32[]{:S(2)}) async-start(f32[8,4,1,16]{3,2,1,0:T(1,128)} %broadcast_in_dim.31), calls=%async_computation.7 | async-start | bytes 32768 | tf_op jit(solution)/shard_map/all_to_all | solution.py:14
  691.2 8.5 %all-to-all-start.11 = ((f32[8,1,128]{2,1,0:T(1,128)}), f32[8,1,128]{2,1,0:T(1,128)S(1)}, u32[]{:S(2)}, u32[]{:S(2)}) async-start(f32[8,1,128]{2,1,0:T(1,128)} %reshape.207), calls=%async_computation.11 | async-start | bytes 8192 | tf_op jit(solution)/shard_map/all_to_all | solution.py:14
  699.7 8.5 %all-to-all-start.3 = ((f32[8,1,128]{2,1,0:T(1,128)}), f32[8,1,128]{2,1,0:T(1,128)S(1)}, u32[]{:S(2)}, u32[]{:S(2)}) async-start(f32[8,1,128]{2,1,0:T(1,128)} %reshape.195), calls=%async_computation.3 | async-start | bytes 8192 | tf_op jit(solution)/shard_map/all_to_all | solution.py:14
  (3 other events, 2.8 us)
Sparse Core Ops, SparseCore 0:
  60.9 262.6 all-reduce.10
  411.9 257.6 all-reduce.8
where the time goes:
time: 719 us; the launch traced here: 717 us
  waiting for transfers between devices  439 us (61%)
  blocking collectives  114 us (16%)
  starting transfers between devices  80.4 us (11%)
  other arithmetic  32.7 us (5%)
  local copies, waits for them, and re-layouts  22.5 us (3%)
  matrix products  14.6 us (2%)
  between operations  14.3 us (2%)
    psum x2, waiting for transfers between devices, body(): raw_sums = lax.psum(right_partial, ROW)  406 us
    psum x4, blocking collectives, over_axes(): shard = lax.psum(shard, axis)  114 us
    all_to_all x12, starting transfers between devices, copy_for_each(): lax.all_to_all(jnp.broadcast_to(shard[None], (length, *shard.shape)), axi...  80.4 us
    all_to_all x12, waiting for transfers between devices, copy_for_each(): lax.all_to_all(jnp.broadcast_to(shard[None], (length, *shard.shape)), axi...  32.5 us
    unnamed x42, local copies, waits for them, and re-layouts  14.8 us
  transfers between devices with their start and end apart: 14, of which 13 were waited for; matrix products, arithmetic and copies ran while one was open for 7% of the time, Pallas kernels for 0%

commit v1 on v0

--- a/solution.py
+++ b/solution.py
@@ -55,7 +55,7 @@
                 for weight, left in zip(weights, left_vecs)
             )
         )
-        raw_sums = lax.psum(right_partial, ROW)
+        raw_sums = lax.psum(lax.psum(right_partial, "row_1"), "row_0")
         right_sums = tuple(
             (
                 raw * left_factor(total, weight)

time: 719 us -> 581 us (0.81)
  waiting for transfers between devices: 439 us -> 300 us
    psum x2 -> x4, waiting for transfers between devices: 406 us -> 267 us  [body(): raw_sums = lax.psum(lax.psum(right_partial, 'row_1'), 'row_0')]
  transfers between devices with their start and end apart: 14 -> 16, of which waited for: 13 -> 15; matrix products, arithmetic and copies ran while one was open for 7% -> 9% of each run, Pallas kernels for 0% -> 0%
where the time goes in v1:
time: 581 us; the launch traced here: 579 us
  waiting for transfers between devices  300 us (52%)
  blocking collectives  115 us (20%)
  starting transfers between devices  79.4 us (14%)
  other arithmetic  32.7 us (6%)
  local copies, waits for them, and re-layouts  22.5 us (4%)
  matrix products  14.6 us (3%)
  between operations  14 us (2%)
    psum x4, waiting for transfers between devices, body(): raw_sums = lax.psum(lax.psum(right_partial, 'row_1'), 'row_0')  267 us
    psum x4, blocking collectives, over_axes(): shard = lax.psum(shard, axis)  115 us
    all_to_all x12, starting transfers between devices, copy_for_each(): lax.all_to_all(jnp.broadcast_to(shard[None], (length, *shard.shape)), axi...  79.3 us
    all_to_all x12, waiting for transfers between devices, copy_for_each(): lax.all_to_all(jnp.broadcast_to(shard[None], (length, *shard.shape)), axi...  32.5 us
    unnamed x42, local copies, waits for them, and re-layouts  14.8 us
    all_to_all x8, other arithmetic, copy_for_each(): lax.all_to_all(jnp.broadcast_to(shard[None], (length, *shard.shape)), axi...  12.1 us
  transfers between devices with their start and end apart: 16, of which 15 were waited for; matrix products, arithmetic and copies ran while one was open for 9% of the time, Pallas kernels for 0%

profile of v1, /device:TPU:1, one launch (start us, length us, event | category | flops | bytes accessed | tf_op | source)
XLA Modules:
  0.0 578.7 jit_solution(8544331438257606731)
XLA Ops:
  9.9 10.1 %all-to-all-start.4 = ((f32[8,1,4096]{2,1,0:T(1,128)}), f32[8,1,4096]{2,1,0:T(1,128)S(1)}, u32[]{:S(2)}, u32[]{:S(2)}) async-start(f32[8,1,4096]{2,1,0:T(1,128)} %reshape.197), calls=%async_computation.4 | async-start | bytes 262144 | tf_op jit(solution)/shard_map/all_to_all | solution.py:14
  21.3 3.9 all-to-all-done.4
  25.2 4.2 all-to-all-start.8
  30.7 5.2 all-to-all-done.8
  38.1 5.1 all-to-all-start
  60.8 58.0 %all-reduce.19.cloned.1.call-done = (f32[4,2,16,512]{3,2,1,0:T(8,128)}, f32[4,1,16,1792]{3,2,0,1:T(8,128)}, f32[4,2,16,512]{3,2,1,0:T(8,128)}) async-done(((f32[4,2,16,512]{3,2,1,0:T(8,128)}, f32[4,1,16,1792]{3,2,0,1:T(8,128)}, f32[4,2,16,512]{3,2,1,0:T(8,128)}), (f32[4,2,16,512]{3,2,1,0:T(8,128)}, f32[4,1,16,1792]{3,2,0,1:T(8,128)}, f32[4,2,16,512]{3,2,1,0:T(8,128)})) %all-reduce.19.cloned.1.call-update) | async-done | bytes 983056 | tf_op jit(solution)/shard_map/psum | solution.py:58
  119.1 44.1 %all-reduce.1 = (f32[4,2,16]{2,1,0:T(2,128)S(1)}, f32[4,1,16]{2,0,1:T(4,128)S(1)}, f32[4,2,16]{2,1,0:T(2,128)S(1)}) all-reduce(f32[4,2,16]{2,1,0:T(2,128)S(1)} %multiply_reduce_fusion.7, f32[4,1,16]{2,0,1:T(4,128)S(1)} %bitcast.30, f32[4,2,16]{2,1,0:T(2,128)S(1)} %multiply_reduce_fusion.9), channel_id=1, replica_groups=mesh['row_0'=16,'row_1'=4,'col'=8] {'row_0'}, use_global_device_ids=true, to_apply=%region_4.0 | all-reduce | flops 320 | bytes 2560 | tf_op jit(solution)/shard_map/psum | solution.py:26
  163.2 13.8 %all-reduce.5 = (f32[4,2,16]{2,1,0:T(2,128)S(1)}, f32[4,1,16]{2,0,1:T(4,128)S(1)}, f32[4,2,16]{2,1,0:T(2,128)S(1)}) all-reduce(f32[4,2,16]{2,1,0:T(2,128)S(1)} %get-tuple-element.9, f32[4,1,16]{2,0,1:T(4,128)S(1)} %get-tuple-element.10, f32[4,2,16]{2,1,0:T(2,128)S(1)} %get-tuple-element.11), channel_id=1, replica_groups=mesh['row_0'=16,'row_1'=4,'col'=8] {'row_1'}, use_global_device_ids=true, to_apply=%region_5.0 | all-reduce | flops 320 | bytes 2560 | tf_op jit(solution)/shard_map/psum | solution.py:26
  177.1 77.6 %all-reduce.15.cloned.1.call-done = (f32[4,2,16,512]{3,2,1,0:T(8,128)}, f32[4,1,16,1792]{3,2,0,1:T(8,128)}, f32[4,2,16,512]{3,2,1,0:T(8,128)}) async-done(((f32[4,2,16,512]{3,2,1,0:T(8,128)}, f32[4,1,16,1792]{3,2,0,1:T(8,128)}, f32[4,2,16,512]{3,2,1,0:T(8,128)}), (f32[4,2,16,512]{3,2,1,0:T(8,128)}, f32[4,1,16,1792]{3,2,0,1:T(8,128)}, f32[4,2,16,512]{3,2,1,0:T(8,128)})) %all-reduce.15.cloned.1.call-update) | async-done | bytes 983056 | tf_op jit(solution)/shard_map/psum | solution.py:58
  256.5 14.5 %all-to-all-start.5 = ((f32[8,4,1,16]{3,2,1,0:T(1,128)}), f32[8,4,1,16]{3,2,1,0:T(1,128)S(1)}, u32[]{:S(2)}, u32[]{:S(2)}) async-start(f32[8,4,1,16]{3,2,1,0:T(1,128)} %broadcast_in_dim.29), calls=%async_computation.5 | async-start | bytes 32768 | tf_op jit(solution)/shard_map/all_to_all | solution.py:14
  275.7 3.9 all-to-all-start.9
  284.7 4.3 all-to-all-start.1
  296.0 4.8 all-to-all-start.6
  306.2 4.8 all-to-all-start.10
  312.2 5.3 all-to-all-done.10
  319.6 5.1 all-to-all-start.2
  333.9 6.0 %all-to-all-done.2 = f32[8,4,2,16,224]{4,3,2,1,0:T(8,128)} async-done(((f32[8,4,2,16,224]{4,3,2,1,0:T(8,128)}), f32[8,4,2,16,224]{4,3,2,1,0:T(8,128)}, u32[]{:S(2)}, u32[]{:S(2)}) %all-to-all-start.2) | async-done | bytes 917536 | tf_op jit(solution)/shard_map/all_to_all | solution.py:14
  342.3 54.0 %all-reduce.17.cloned.1.call-done = (f32[4,2,16,512]{3,2,1,0:T(8,128)}, f32[4,1,16,1792]{3,2,0,1:T(8,128)}, f32[4,2,16,512]{3,2,1,0:T(8,128)}) async-done(((f32[4,2,16,512]{3,2,1,0:T(8,128)}, f32[4,1,16,1792]{3,2,0,1:T(8,128)}, f32[4,2,16,512]{3,2,1,0:T(8,128)}), (f32[4,2,16,512]{3,2,1,0:T(8,128)}, f32[4,1,16,1792]{3,2,0,1:T(8,128)}, f32[4,2,16,512]{3,2,1,0:T(8,128)})) %all-reduce.17.cloned.1.call-update) | async-done | bytes 983056 | tf_op jit(solution)/shard_map/psum | solution.py:58
  396.7 44.0 %all-reduce = (f32[4,2,16]{2,1,0:T(2,128)S(1)}, f32[4,1,16]{2,0,1:T(4,128)S(1)}, f32[4,2,16]{2,1,0:T(2,128)S(1)}) all-reduce(f32[4,2,16]{2,1,0:T(2,128)S(1)} %multiply_reduce_fusion.6, f32[4,1,16]{2,0,1:T(4,128)S(1)} %bitcast.31, f32[4,2,16]{2,1,0:T(2,128)S(1)} %multiply_reduce_fusion.8), channel_id=1, replica_groups=mesh['row_0'=16,'row_1'=4,'col'=8] {'row_0'}, use_global_device_ids=true, to_apply=%region_12.0 | all-reduce | flops 320 | bytes 2560 | tf_op jit(solution)/shard_map/psum | solution.py:26
  440.7 13.5 %all-reduce.4 = (f32[4,2,16]{2,1,0:T(2,128)S(1)}, f32[4,1,16]{2,0,1:T(4,128)S(1)}, f32[4,2,16]{2,1,0:T(2,128)S(1)}) all-reduce(f32[4,2,16]{2,1,0:T(2,128)S(1)} %get-tuple-element.6, f32[4,1,16]{2,0,1:T(4,128)S(1)} %get-tuple-element.7, f32[4,2,16]{2,1,0:T(2,128)S(1)} %get-tuple-element.8), channel_id=1, replica_groups=mesh['row_0'=16,'row_1'=4,'col'=8] {'row_1'}, use_global_device_ids=true, to_apply=%region_13.0 | all-reduce | flops 320 | bytes 2560 | tf_op jit(solution)/shard_map/psum | solution.py:26
  454.3 77.8 %all-reduce.13.cloned.1.call-done = (f32[4,2,16,512]{3,2,1,0:T(8,128)}, f32[4,1,16,1792]{3,2,0,1:T(8,128)}, f32[4,2,16,512]{3,2,1,0:T(8,128)}) async-done(((f32[4,2,16,512]{3,2,1,0:T(8,128)}, f32[4,1,16,1792]{3,2,0,1:T(8,128)}, f32[4,2,16,512]{3,2,1,0:T(8,128)}), (f32[4,2,16,512]{3,2,1,0:T(8,128)}, f32[4,1,16,1792]{3,2,0,1:T(8,128)}, f32[4,2,16,512]{3,2,1,0:T(8,128)})) %all-reduce.13.cloned.1.call-update) | async-done | bytes 983056 | tf_op jit(solution)/shard_map/psum | solution.py:58
  533.9 14.5 %all-to-all-start.7 = ((f32[8,4,1,16]{3,2,1,0:T(1,128)}), f32[8,4,1,16]{3,2,1,0:T(1,128)S(1)}, u32[]{:S(2)}, u32[]{:S(2)}) async-start(f32[8,4,1,16]{3,2,1,0:T(1,128)} %broadcast_in_dim.31), calls=%async_computation.7 | async-start | bytes 32768 | tf_op jit(solution)/shard_map/all_to_all | solution.py:14
  553.1 3.9 all-to-all-start.11
  561.6 3.9 all-to-all-start.3
  (129 shorter events, 82.1 us)
Async XLA Ops:
  7.2 22.3 %copy-start = (bf16[4,2,224,512]{3,2,1,0:T(8,128)(2,1)S(1)}, bf16[4,2,224,512]{3,2,1,0:T(8,128)(2,1)}, u32[]{:S(2)}) copy-start(bf16[4,2,224,512]{3,2,1,0:T(8,128)(2,1)} %param.6) | copy-start | bytes 5505028
  9.0 20.4 %copy-start.10 = (bf16[4,2,16,512]{3,2,1,0:T(8,128)(2,1)S(1)}, bf16[4,2,16,512]{3,2,1,0:T(8,128)(2,1)}, u32[]{:S(2)}) copy-start(bf16[4,2,16,512]{3,2,1,0:T(8,128)(2,1)} %param.9) | copy-start | bytes 393220
  9.9 15.4 %all-to-all-start.4 = ((f32[8,1,4096]{2,1,0:T(1,128)}), f32[8,1,4096]{2,1,0:T(1,128)S(1)}, u32[]{:S(2)}, u32[]{:S(2)}) async-start(f32[8,1,4096]{2,1,0:T(1,128)} %reshape.197), calls=%async_computation.4 | async-start | bytes 262144 | tf_op jit(solution)/shard_map/all_to_all | solution.py:14
  25.2 10.7 %all-to-all-start.8 = ((f32[8,1,8192]{2,1,0:T(1,128)}), f32[8,1,8192]{2,1,0:T(1,128)S(1)}, u32[]{:S(2)}, u32[]{:S(2)}) async-start(f32[8,1,8192]{2,1,0:T(1,128)} %reshape.201), calls=%async_computation.8 | async-start | bytes 524288 | tf_op jit(solution)/shard_map/all_to_all | solution.py:14
  30.7 18.8 %copy-start.1 = (bf16[4,64,1792]{2,1,0:T(8,128)(2,1)S(1)}, bf16[4,64,1792]{2,1,0:T(8,128)(2,1)}, u32[]{:S(2)}) copy-start(bf16[4,64,1792]{2,1,0:T(8,128)(2,1)} %param.7) | copy-start | bytes 2752516
  38.1 20.2 %all-to-all-start = ((f32[8,4,2,16,224]{4,3,2,1,0:T(8,128)}), f32[8,4,2,16,224]{4,3,2,1,0:T(8,128)}, u32[]{:S(2)}, u32[]{:S(2)}) async-start(f32[8,4,2,16,224]{4,3,2,1,0:T(8,128)} %broadcast_in_dim.24), calls=%async_computation | async-start | bytes 2097152 | tf_op jit(solution)/shard_map/all_to_all | solution.py:14
  43.2 75.6 %all-reduce.19.cloned.1.call-start = ((), (), s32[]{:S(2)}) async-start(), calls=%async_computation.15 | async-start | bytes 1966080 | tf_op jit(solution)/shard_map/psum | solution.py:58
  59.7 59.1 %copy-start.8 = (f32[4,16,64]{2,1,0:T(8,128)S(1)}, f32[4,16,64]{2,1,0:T(8,128)}, u32[]{:S(2)}) copy-start(f32[4,16,64]{2,1,0:T(8,128)} %reduce_sum.228) | copy-start | bytes 49156
  60.7 193.9 %all-reduce.15.cloned.1.call-start = ((), (), s32[]{:S(2)}) async-start(), calls=%async_computation.13 | async-start | bytes 1966080 | tf_op jit(solution)/shard_map/psum | solution.py:58
  256.5 19.2 %all-to-all-start.5 = ((f32[8,4,1,16]{3,2,1,0:T(1,128)}), f32[8,4,1,16]{3,2,1,0:T(1,128)S(1)}, u32[]{:S(2)}, u32[]{:S(2)}) async-start(f32[8,4,1,16]{3,2,1,0:T(1,128)} %broadcast_in_dim.29), calls=%async_computation.5 | async-start | bytes 32768 | tf_op jit(solution)/shard_map/all_to_all | solution.py:14
  275.7 8.5 %all-to-all-start.9 = ((f32[8,1,128]{2,1,0:T(1,128)}), f32[8,1,128]{2,1,0:T(1,128)S(1)}, u32[]{:S(2)}, u32[]{:S(2)}) async-start(f32[8,1,128]{2,1,0:T(1,128)} %reshape.203), calls=%async_computation.9 | async-start | bytes 8192 | tf_op jit(solution)/shard_map/all_to_all | solution.py:14
  281.8 29.1 %copy-start.3 = (f32[4,2,16,512]{3,2,1,0:T(8,128)S(1)}, f32[4,2,16,512]{3,2,1,0:T(8,128)}, u32[]{:S(2)}) copy-start(f32[4,2,16,512]{3,2,1,0:T(8,128)} %get-tuple-element.15) | copy-start | bytes 786436
  284.7 11.3 %all-to-all-start.1 = ((f32[8,1,128]{2,1,0:T(1,128)}), f32[8,1,128]{2,1,0:T(1,128)S(1)}, u32[]{:S(2)}, u32[]{:S(2)}) async-start(f32[8,1,128]{2,1,0:T(1,128)} %reshape.193), calls=%async_computation.1 | async-start | bytes 8192 | tf_op jit(solution)/shard_map/all_to_all | solution.py:14
  296.0 10.2 %all-to-all-start.6 = ((f32[8,1,4096]{2,1,0:T(1,128)}), f32[8,1,4096]{2,1,0:T(1,128)}, u32[]{:S(2)}, u32[]{:S(2)}) async-start(f32[8,1,4096]{2,1,0:T(1,128)} %reshape.199), calls=%async_computation.6 | async-start | bytes 262144 | tf_op jit(solution)/shard_map/all_to_all | solution.py:14
  306.2 11.4 %all-to-all-start.10 = ((f32[8,1,8192]{2,1,0:T(1,128)}), f32[8,1,8192]{2,1,0:T(1,128)}, u32[]{:S(2)}, u32[]{:S(2)}) async-start(f32[8,1,8192]{2,1,0:T(1,128)} %reshape.205), calls=%async_computation.10 | async-start | bytes 524288 | tf_op jit(solution)/shard_map/all_to_all | solution.py:14
  319.6 20.2 %all-to-all-start.2 = ((f32[8,4,2,16,224]{4,3,2,1,0:T(8,128)}), f32[8,4,2,16,224]{4,3,2,1,0:T(8,128)}, u32[]{:S(2)}, u32[]{:S(2)}) async-start(f32[8,4,2,16,224]{4,3,2,1,0:T(8,128)} %broadcast_in_dim.26), calls=%async_computation.2 | async-start | bytes 2097152 | tf_op jit(solution)/shard_map/all_to_all | solution.py:14
  324.7 71.6 %all-reduce.17.cloned.1.call-start = ((), (), s32[]{:S(2)}) async-start(), calls=%async_computation.14 | async-start | bytes 1966080 | tf_op jit(solution)/shard_map/psum | solution.py:58
  341.2 55.2 %copy-start.9 = (f32[4,16,64]{2,1,0:T(8,128)S(1)}, f32[4,16,64]{2,1,0:T(8,128)}, u32[]{:S(2)}) copy-start(f32[4,16,64]{2,1,0:T(8,128)} %reduce_sum.233) | copy-start | bytes 49156
  342.3 189.8 %all-reduce.13.cloned.1.call-start = ((), (), s32[]{:S(2)}) async-start(), calls=%async_computation.12 | async-start | bytes 1966080 | tf_op jit(solution)/shard_map/psum | solution.py:58
  532.0 34.8 %copy-start.6 = (f32[4,2,16,512]{3,2,1,0:T(8,128)S(1)}, f32[4,2,16,512]{3,2,1,0:T(8,128)}, u32[]{:S(2)}) copy-start(f32[4,2,16,512]{3,2,1,0:T(8,128)} %get-tuple-element.14) | copy-start | bytes 786436
  532.0 39.3 %copy-start.5 = (f32[4,2,16,512]{3,2,1,0:T(8,128)S(1)}, f32[4,2,16,512]{3,2,1,0:T(8,128)}, u32[]{:S(2)}) copy-start(f32[4,2,16,512]{3,2,1,0:T(8,128)} %get-tuple-element.12) | copy-start | bytes 786436
  533.9 19.2 %all-to-all-start.7 = ((f32[8,4,1,16]{3,2,1,0:T(1,128)}), f32[8,4,1,16]{3,2,1,0:T(1,128)S(1)}, u32[]{:S(2)}, u32[]{:S(2)}) async-start(f32[8,4,1,16]{3,2,1,0:T(1,128)} %broadcast_in_dim.31), calls=%async_computation.7 | async-start | bytes 32768 | tf_op jit(solution)/shard_map/all_to_all | solution.py:14
  553.1 8.5 %all-to-all-start.11 = ((f32[8,1,128]{2,1,0:T(1,128)}), f32[8,1,128]{2,1,0:T(1,128)S(1)}, u32[]{:S(2)}, u32[]{:S(2)}) async-start(f32[8,1,128]{2,1,0:T(1,128)} %reshape.207), calls=%async_computation.11 | async-start | bytes 8192 | tf_op jit(solution)/shard_map/all_to_all | solution.py:14
  561.6 8.5 %all-to-all-start.3 = ((f32[8,1,128]{2,1,0:T(1,128)}), f32[8,1,128]{2,1,0:T(1,128)S(1)}, u32[]{:S(2)}, u32[]{:S(2)}) async-start(f32[8,1,128]{2,1,0:T(1,128)} %reshape.195), calls=%async_computation.3 | async-start | bytes 8192 | tf_op jit(solution)/shard_map/all_to_all | solution.py:14
  (5 other events, 42.3 us)
Sparse Core Ops, SparseCore 0:
  60.9 57.8 all-reduce.18
  121.3 133.2 all-reduce.14
  342.4 53.8 all-reduce.16
  398.7 133.2 all-reduce.12
